TPU v7x, 32 devices: a whole 2x2x4 slice. The times are simulated.
32 devices in a mesh: lon: 8 (over y, x, core), lev: 4 (over z).
Axes of the slice: x: 2, y: 2, z: 4, core: 2. Of those that a mesh axis runs over, the one named last changes fastest.
Arguments:
- field: float32 [72, 128, 128], P('lev', 'lon'), may hold values from -6 to 6
- ens: bfloat16 [80, 72, 128, 128], P(None, 'lev', 'lon'), may hold values from -2 to 2
- sdev: float32 [72, 128, 128], P('lev', 'lon'), may hold values from 0.5 to 2
- lon_taper: bfloat16 [17], replicated, may hold values from 0 to 0.079589844
- static_taper: bfloat16 [17], replicated, may hold values from 0 to 0.079589844
- loc_vert: bfloat16 [72, 72], P('lev'), may hold values from -0.75 to 0.75
- static_vert: bfloat16 [72, 72], P('lev'), may hold values from -0.75 to 0.75
- obs_block: int32 [8192], P('lon'), may hold values from -1 to 127, as said below
- obs_value: float32 [8192], P('lon'), may hold values from -6 to 6
- obs_rinv: float32 [8192], P('lon'), may hold values from 0.25 to 4
- obs_horiz: float32 [8192, 128], P('lon'), may hold values from -0.5 to 0.5
- obs_vert: float32 [8192, 72], P('lon', 'lev'), may hold values from -0.75 to 0.75
Outputs:
- increment: float32 [72, 128, 128], P('lev', 'lon')
- adjoint_field: float32 [72, 128, 128], P('lev', 'lon')
- obs_cost: float32 [], replicated
Inputs may be any that keep to these rules, and one draw needn't show every extreme that they name: `obs_block`: each longitude sector's 1024 slots name only blocks within that sector's longitudes; live slots come first, in non-falling block order; at least half of a sector's slots are live, and some sector has all its slots live.
All inputs are finite; a program needn't handle non-finite values.
Results may differ from a plain program's by a relative error of at most 0.0041.
Values may be sent and summed in bfloat16 or wider, within the bound.
A program may use at most 128 MiB of HBM per device.

v0:
```python
import functools

import jax
import jax.numpy as jnp
from jax import lax
from jax.experimental import pallas as pl
from jax.experimental.pallas import tpu as pltpu
from jax.sharding import PartitionSpec as P

ens_weight = 0.8
static_weight = 0.5
MESH = pl.DeviceIdType.MESH
F32 = jnp.float32
BF16 = jnp.bfloat16


def split(values):
    high = values.astype(BF16)
    return high, (values - high.astype(F32)).astype(BF16)


def swap_groups(source, target, count, lats):
    group = lax.broadcasted_iota(jnp.int32, (count, lats), 1) // 16
    for by in range(8):
        rows = jnp.zeros((count, lats), F32)
        for s in range(8):
            line = source[pl.ds(s, count, stride=8)]
            shift = (16 * (s - by)) % lats
            moved = pltpu.roll(line, shift, 1) if shift else line
            rows = jnp.where(group == s, moved, rows)
        target[pl.ds(by, count, stride=8)] = rows


def main_kernel(
    dims,
    ens,
    field,
    sdev,
    taper,
    static_taper,
    loc,
    svert,
    ids,
    value,
    rinv,
    horiz,
    vert,
    out,
    adj,
    cost,
    ebuf,
    zbuf,
    hsend,
    fbuf,
    spart,
    zs,
    ssend,
    lpad,
    spad,
    lg,
    spread,
    w,
    ws,
    pick,
    tband,
    acc,
    accb,
    rbuf,
    hhigh,
    hlow,
    blocks,
    part,
    parts,
    costs,
    own_sem,
    ens_send,
    ens_recv,
    halo_send,
    halo_recv,
    small_send,
    small_recv,
    back_send,
    back_recv,
    part_send,
    part_recv,
    cost_send,
    cost_recv,
):
    nlev, nlon, levs, cols, half, pairs = dims
    rows = levs * cols
    full = nlev * rows
    edge = nlev * levs * half
    wide = full + 2 * edge
    me = lax.axis_index("lev")
    lon = lax.axis_index("lon")
    right, left = lax.rem(lon + 1, nlon), lax.rem(lon + nlon - 1, nlon)
    peers = [lax.rem(me + off, nlev) for off in range(1, nlev)]
    sources = [lax.rem(me + nlev - off, nlev) for off in range(1, nlev)]

    def slot(rank):
        return pl.ds(pl.multiple_of(rank * rows, 16), rows)

    own_copy = pltpu.make_async_copy(
        ens.at[pl.ds(me * 2 * pairs, 2 * pairs)], ebuf.at[:, slot(me)], own_sem
    )
    own_copy.start()
    width = loc.shape[1]
    for matrix, padded in ((loc, lpad), (svert, spad)):
        padded[...] = jnp.zeros_like(padded)
        padded[:levs, :width] = matrix[...]
    spart[...] = (sdev[...] * field[...]).astype(BF16)
    lons = [lax.rem(lon + off, nlon) for off in range(1, nlon)]

    barrier = pltpu.get_barrier_semaphore()
    for peer in peers:
        pl.semaphore_signal(barrier, inc=1, device_id={"lev": peer}, device_id_type=MESH)
    for peer in lons:
        pl.semaphore_signal(barrier, inc=1, device_id={"lon": peer}, device_id_type=MESH)
    pl.semaphore_wait(barrier, nlev + nlon - 2)

    def small(which, off, peer, rank):
        src, dst = ((lpad, lg), (field, fbuf), (spart, zs))[which]
        return pltpu.make_async_remote_copy(
            src_ref=src,
            dst_ref=dst.at[rank] if which == 0 else dst.at[slot(rank)],
            send_sem=small_send.at[which, off],
            recv_sem=small_recv.at[which, off],
            device_id={"lev": peer},
            device_id_type=MESH,
        )

    def ens_copy(off, peer, rank, c):
        return pltpu.make_async_remote_copy(
            src_ref=ens.at[peer * 2 * pairs + c],
            dst_ref=ebuf.at[c, slot(rank)],
            send_sem=ens_send.at[off, c],
            recv_sem=ens_recv.at[off, c],
            device_id={"lev": peer},
            device_id_type=MESH,
        )

    def halo_copy(side, c, h):
        at = pl.ds(h * 128, 128)
        return pltpu.make_async_remote_copy(
            src_ref=hsend.at[side, c, :, at],
            dst_ref=zbuf.at[c, pl.ds(full + side * edge, edge), at],
            send_sem=halo_send.at[side, 2 * c + h],
            recv_sem=halo_recv.at[side, 2 * c + h],
            device_id={"lon": (right, left)[side]},
            device_id_type=MESH,
        )

    def static_halo(side):
        return pltpu.make_async_remote_copy(
            src_ref=ssend.at[side],
            dst_ref=zs.at[pl.ds(full + side * edge, edge)],
            send_sem=halo_send.at[side, 2 * pairs],
            recv_sem=halo_recv.at[side, 2 * pairs],
            device_id={"lon": (right, left)[side]},
            device_id_type=MESH,
        )

    def back_copy(off, peer):
        return pltpu.make_async_remote_copy(
            src_ref=accb.at[slot(peer)],
            dst_ref=rbuf.at[off],
            send_sem=back_send.at[off],
            recv_sem=back_recv.at[off],
            device_id={"lev": peer},
            device_id_type=MESH,
        )

    def part_copy(off, peer, rank):
        return pltpu.make_async_remote_copy(
            src_ref=part,
            dst_ref=parts.at[rank],
            send_sem=part_send.at[off],
            recv_sem=part_recv.at[off],
            device_id={"lev": peer},
            device_id_type=MESH,
        )

    def cost_copy(off, rank):
        return pltpu.make_async_remote_copy(
            src_ref=costs.at[lon],
            dst_ref=costs.at[rank],
            send_sem=cost_send.at[off],
            recv_sem=cost_recv.at[off],
            device_id={"lon": lons[off]},
            device_id_type=MESH,
        )

    for which in range(2):
        for off, peer in enumerate(peers):
            small(which, off, peer, me).start()

    def send_chunk(c, carry):
        for off, peer in enumerate(peers):
            ens_copy(off, peer, me, c).start()
        return carry

    lax.fori_loop(0, 2 * pairs, send_chunk, 0)
    for off, peer in enumerate(peers):
        small(2, off, peer, me).start()

    lg[me] = lpad[...]
    fbuf[slot(me)] = field[...]
    zs[slot(me)] = spart[...]
    acc[...] = jnp.zeros_like(acc)

    lanes = lpad.shape[1]
    col = lax.broadcasted_iota(jnp.int32, (lanes, wide), 1)
    row = lax.broadcasted_iota(jnp.int32, (lanes, wide), 0)
    inner = col < full
    low = col < full + edge
    tail = jnp.where(low, col - full, col - full - edge)
    level = jnp.where(inner, col // cols, tail // half)
    place = jnp.where(
        inner, half + col % cols, jnp.where(low, tail % half, half + cols + tail % half)
    )
    pick[...] = jnp.where(row == level, 1.0, 0.0).astype(BF16)
    spot = place[:cols] - lax.broadcasted_iota(jnp.int32, (cols, wide), 0)
    for which, weights in enumerate((taper, static_taper)):
        tap = weights[...].astype(F32)
        band = jnp.zeros((cols, wide), F32)
        for d in range(tap.shape[1]):
            band = jnp.where(spot == d, tap[:, d : d + 1], band)
        tband[which * cols : (which + 1) * cols] = band

    padrows = lpad.shape[0]

    def expand(dst, which, rank, first):
        def one(q, carry):
            line = spread[pl.ds(rank * padrows + q, 1)]
            at = pl.ds(pl.multiple_of((first + q) * cols, 16), cols)
            dst[at] = (line * tband[which * cols : (which + 1) * cols]).astype(BF16)
            return carry

        lax.fori_loop(0, levs, one, 0)

    spread[:padrows] = jnp.dot(spad[...], pick[...], preferred_element_type=F32)
    expand(ws, 1, 0, 0)
    hhigh[...], hlow[...] = split(horiz[...])

    for off, rank in enumerate(sources):
        small(0, off, peers[off], rank).wait_recv()

    def expand_loc(rank, carry):
        spread[pl.ds(pl.multiple_of(rank * padrows, 8), padrows)] = jnp.dot(
            lg[rank], pick[...], preferred_element_type=F32
        )
        expand(w, 0, rank, rank * levs)
        return carry

    lax.fori_loop(0, nlev, expand_loc, 0)

    for off, rank in enumerate(sources):
        small(1, off, peers[off], rank).wait_recv()

    def edges(values):
        lines = values.reshape(nlev * levs, cols, values.shape[1])
        to_right = lines[:, cols - half :].reshape(edge, values.shape[1]).astype(BF16)
        to_left = lines[:, :half].reshape(edge, values.shape[1]).astype(BF16)
        return to_right, to_left

    own_copy.wait()

    tile = full // 3 if full % 48 == 0 else full

    def chunk(c, carry):
        @pl.when(c < pairs)
        def _():
            for h in range(2):
                for off, rank in enumerate(sources):
                    ens_copy(off, peers[off], rank, 2 * c + h).wait_recv()
                at = slice(h * 128, (h + 1) * 128)
                product = ebuf[2 * c + h].astype(F32) * fbuf[...]
                hsend[0, c, :, at], hsend[1, c, :, at] = edges(product)
                zbuf[c, :full, at] = product.astype(BF16)
                for side in range(2):
                    halo_copy(side, c, h).start()

        @pl.when(c == pairs)
        def _():
            for off, rank in enumerate(sources):
                small(2, off, peers[off], rank).wait_recv()
            ssend[0], ssend[1] = edges(zs[:full].astype(F32))
            for side in range(2):
                static_halo(side).start()

        @pl.when(c >= 1)
        def _():
            d = c - 1
            for h in range(2):
                for side in range(2):
                    halo_copy(side, d, h).wait_recv()

            def piece(q, inner_carry):
                at = pl.ds(pl.multiple_of(q * tile, 16), tile)
                zv = jnp.dot(w[at], zbuf[d], preferred_element_type=F32)
                acc[at] += (
                    ebuf[2 * d, at].astype(F32) * zv[:, :128]
                    + ebuf[2 * d + 1, at].astype(F32) * zv[:, 128:]
                )
                return inner_carry

            lax.fori_loop(0, full // tile, piece, 0)

        return carry

    lax.fori_loop(0, pairs + 1, chunk, 0)

    accb[...] = acc[...].astype(BF16)
    for side in range(2):
        static_halo(side).wait_recv()
    static = jnp.dot(ws[...], zs[...], preferred_element_type=F32)
    base = static_weight * sdev[...] * static
    out[...] = base
    for off, peer in enumerate(peers):
        back_copy(off, peer).start()
    total = acc[slot(me)]
    for off, peer in enumerate(peers):
        back_copy(off, peer).wait_recv()
        total = total + rbuf[off].astype(F32)
    out[...] = out[...] + ens_weight * total

    count = rows // 8
    lats = out.shape[1]
    nblk = rows // levs
    slots = ids.shape[1]
    contract = (((1,), (1,)), ((), ()))
    local_ids = ids[...] - lon * nblk
    block = lax.broadcasted_iota(jnp.int32, (nblk, slots), 0)
    chosen = (block == local_ids) & (ids[...] >= 0)
    selector = jnp.where(chosen, 1.0, 0.0)
    swap_groups(out, blocks, count, lats)
    high, low_part = split(blocks[...])
    projected = lax.dot_general(high, hhigh[...], contract, preferred_element_type=F32)
    projected += lax.dot_general(low_part, hhigh[...], contract, preferred_element_type=F32)
    projected += lax.dot_general(high, hlow[...], contract, preferred_element_type=F32)
    picked = jnp.sum(projected.reshape(levs, nblk, slots) * selector[None], axis=1)
    mine = jnp.sum(picked * vert[...], axis=0, keepdims=True)
    part[...] = mine
    parts[me] = mine
    for off, peer in enumerate(peers):
        part_copy(off, peer, me).start()
    for off, rank in enumerate(sources):
        part_copy(off, peers[off], rank).wait_recv()
    hx = parts[0]
    for rank in range(1, nlev):
        hx = hx + parts[rank]
    miss = hx - value[...]
    dep = jnp.where(ids[...] >= 0, rinv[...] * miss, 0.0)
    terms = 0.5 * dep * miss
    folded = terms[:, :128]
    for q in range(1, slots // 128):
        folded = folded + terms[:, q * 128 : (q + 1) * 128]
    costs[lon] = folded
    weighted = vert[...] * dep
    spread_obs = (weighted[:, None, :] * selector[None]).reshape(rows, slots)
    high, low_part = split(spread_obs)
    for off in range(nlon - 1):
        cost_copy(off, lon).start()
    sums = jnp.dot(high, hhigh[...], preferred_element_type=F32)
    sums += jnp.dot(low_part, hhigh[...], preferred_element_type=F32)
    sums += jnp.dot(high, hlow[...], preferred_element_type=F32)
    blocks[...] = sums
    swap_groups(blocks, adj, count, lats)
    for off in range(nlon - 1):
        cost_copy(off, lax.rem(lon + nlon - off - 1, nlon)).wait_recv()
    total_cost = costs[0]
    for rank in range(1, nlon):
        total_cost = total_cost + costs[rank]
    cost[...] = jnp.sum(total_cost, axis=1, keepdims=True)
    for off, peer in enumerate(peers):
        part_copy(off, peer, me).wait_send()
    for off in range(nlon - 1):
        cost_copy(off, lon).wait_send()

    for which in range(3):
        for off, peer in enumerate(peers):
            small(which, off, peer, me).wait_send()
    for off, peer in enumerate(peers):
        back_copy(off, peer).wait_send()
    for side in range(2):
        static_halo(side).wait_send()

    def drain(c, carry):
        for h in range(2):
            for off, peer in enumerate(peers):
                ens_copy(off, peer, me, 2 * c + h).wait_send()
            for side in range(2):
                halo_copy(side, c, h).wait_send()
        return carry

    lax.fori_loop(0, pairs, drain, 0)


def body(
    nlev,
    nlon,
    field,
    ens,
    sdev,
    lon_taper,
    static_taper,
    loc_vert,
    static_vert,
    obs_block,
    obs_value,
    obs_rinv,
    obs_horiz,
    obs_vert,
):
    members, levs, cols, lats = ens.shape
    half = lon_taper.shape[0] // 2
    pairs = members // nlev // 2
    rows = levs * cols
    full = nlev * rows
    edge = nlev * levs * half
    wide = full + 2 * edge
    slots = obs_block.shape[0]
    padrows = -(-levs // 16) * 16
    vmem = pl.BlockSpec(memory_space=pltpu.VMEM)
    dma = pltpu.SemaphoreType.DMA
    increment, adjoint_field, obs_cost = pl.pallas_call(
        functools.partial(main_kernel, (nlev, nlon, levs, cols, half, pairs)),
        out_shape=(
            jax.ShapeDtypeStruct((rows, lats), F32),
            jax.ShapeDtypeStruct((rows, lats), F32),
            jax.ShapeDtypeStruct((1, 1), F32),
        ),
        in_specs=[pl.BlockSpec(memory_space=pl.ANY)] + [vmem] * 11,
        out_specs=(vmem, vmem, vmem),
        scratch_shapes=[
            pltpu.VMEM((2 * pairs, full, lats), BF16),
            pltpu.VMEM((pairs, wide, 2 * lats), BF16),
            pltpu.VMEM((2, pairs, edge, 2 * lats), BF16),
            pltpu.VMEM((full, lats), F32),
            pltpu.VMEM((rows, lats), BF16),
            pltpu.VMEM((wide, lats), BF16),
            pltpu.VMEM((2, edge, lats), BF16),
            pltpu.VMEM((padrows, 128), BF16),
            pltpu.VMEM((padrows, 128), BF16),
            pltpu.VMEM((nlev, padrows, 128), BF16),
            pltpu.VMEM((nlev * padrows, wide), F32),
            pltpu.VMEM((full, wide), BF16),
            pltpu.VMEM((rows, wide), BF16),
            pltpu.VMEM((128, wide), BF16),
            pltpu.VMEM((2 * cols, wide), F32),
            pltpu.VMEM((full, lats), F32),
            pltpu.VMEM((full, lats), BF16),
            pltpu.VMEM((nlev - 1, rows, lats), BF16),
            pltpu.VMEM((slots, lats), BF16),
            pltpu.VMEM((slots, lats), BF16),
            pltpu.VMEM((rows, lats), F32),
            pltpu.VMEM((1, slots), F32),
            pltpu.VMEM((nlev, 1, slots), F32),
            pltpu.VMEM((nlon, 1, 128), F32),
            dma,
            dma((nlev - 1, 2 * pairs)),
            dma((nlev - 1, 2 * pairs)),
            dma((2, 2 * pairs + 1)),
            dma((2, 2 * pairs + 1)),
            dma((3, nlev - 1)),
            dma((3, nlev - 1)),
            dma((nlev - 1,)),
            dma((nlev - 1,)),
            dma((nlev - 1,)),
            dma((nlev - 1,)),
            dma((nlon - 1,)),
            dma((nlon - 1,)),
        ],
        compiler_params=pltpu.CompilerParams(
            collective_id=0, has_side_effects=True, vmem_limit_bytes=60 * 1024 * 1024
        ),
        name="covariance",
    )(
        ens.reshape(members, rows, lats),
        field.reshape(rows, lats),
        sdev.reshape(rows, lats),
        lon_taper.reshape(1, -1),
        static_taper.reshape(1, -1),
        loc_vert,
        static_vert,
        obs_block.reshape(1, slots),
        obs_value.reshape(1, slots),
        obs_rinv.reshape(1, slots),
        obs_horiz,
        obs_vert.T,
    )
    shape = (levs, cols, lats)
    return (increment.reshape(shape), adjoint_field.reshape(shape), obs_cost[0, 0])


def solution(mesh):
    return jax.shard_map(
        functools.partial(body, mesh.shape["lev"], mesh.shape["lon"]),
        mesh=mesh,
        in_specs=(
            P("lev", "lon", None),
            P(None, "lev", "lon", None),
            P("lev", "lon", None),
            P(),
            P(),
            P("lev", None),
            P("lev", None),
            P("lon"),
            P("lon"),
            P("lon"),
            P("lon", None),
            P("lon", "lev"),
        ),
        out_specs=(P("lev", "lon", None), P("lev", "lon", None), P()),
        check_vma=False,
    )
```

profile of v0, /device:TPU:0, one launch (start us, length us, event | category | flops | bytes accessed | tf_op | source)
XLA Modules:
  0.0 184.3 jit_solution(1148757204537434068)
XLA Ops:
  0.6 178.6 %covariance.1 = (f32[288,128]{1,0:T(8,128)}, f32[288,128]{1,0:T(8,128)}, f32[1,1]{1,0:T(1,128)}) custom-call(bf16[80,288,128]{2,1,0:T(8,128)(2,1)} %bitcast.12, f32[288,128]{1,0:T(8,128)} %bitcast.13, f32[288,128]{1,0:T(8,128)} %bitcast.14, bf16[1,17]{1,0:T(2,128)(2,1)} %bitcast.21, bf16[1,17]{1,0:T(2,128)(2,1)} %bitcast.22, bf16[18,72]{1,0:T(8,128)(2,1)} %loc.1, ...), custom_call_target="tpu_custom_call" | custom-call | tf_op jit(solution)/shard_map/covariance/pallas_call | solution.py:426
  179.3 1.6 copy.18
  180.9 1.6 copy.19
where the time goes:
time: 184 us
  Pallas kernels  179 us (97%)
  local copies, waits for them, and re-layouts  3.16 us (2%)
  between operations  2.46 us (1%)
    pallas_call x1, Pallas kernels, body(): pl.pallas_call(functools.partial(main_kernel, (nlev, nlon, levs, cols, ha...  179 us

commit v1 on v0

v1 whole, which is shorter than its diff:
```python
import functools

import jax
import jax.numpy as jnp
from jax import lax
from jax.experimental import pallas as pl
from jax.experimental.pallas import tpu as pltpu
from jax.sharding import PartitionSpec as P

ens_weight = 0.8
static_weight = 0.5
MESH = pl.DeviceIdType.MESH
F32 = jnp.float32
BF16 = jnp.bfloat16


LINE = 8
GROUP = 16
LEAD = 0


def main_kernel(
    dims,
    ens,
    field_in,
    sdev_in,
    taper_in,
    static_taper_in,
    loc_in,
    svert_in,
    ids_in,
    value_in,
    rinv_in,
    horiz_in,
    vert_in,
    both,
    cost,
    field,
    sdev,
    taper,
    static_taper,
    loc,
    svert,
    ids,
    value,
    rinv,
    horiz,
    vert,
    ebuf,
    zbuf,
    hsend,
    fsend,
    fgroup,
    fbuf,
    spart,
    sband,
    sbuf,
    ssend,
    smooth,
    zs,
    lpad,
    spad,
    lg,
    spread,
    w,
    ws,
    pick,
    tband,
    acc,
    accb,
    rbuf,
    hturn,
    hcol,
    hrow,
    cells,
    vfold,
    vsend,
    vg,
    vx,
    part,
    parts,
    costs,
    own_sem,
    in_sem,
    ens_send,
    ens_recv,
    halo_send,
    halo_recv,
    small_send,
    small_recv,
    relay_send,
    back_send,
    back_recv,
    part_send,
    part_recv,
    cost_send,
    cost_recv,
):
    nlev, nlon, levs, cols, half, pairs = dims
    rows = levs * cols
    full = nlev * rows
    edge = nlev * levs * half
    wide = full + 2 * edge
    lead = min(LEAD, pairs)
    strip = levs * half
    hl = nlev // 2
    me = lax.axis_index("lev")
    lon = lax.axis_index("lon")
    right, left = lax.rem(lon + 1, nlon), lax.rem(lon + nlon - 1, nlon)
    peers = [lax.rem(me + off, nlev) for off in range(1, nlev)]
    sources = [lax.rem(me + nlev - off, nlev) for off in range(1, nlev)]
    side = me // hl
    gate = (me == hl - 1) | (me == hl)
    other_gate = hl - 1 + (1 - side)
    far_ranks = [(1 - side) * hl + q for q in range(hl)]
    near_ranks = [side * hl + lax.rem(me - side * hl + q, hl) for q in range(1, hl)]

    def slot(rank):
        return pl.ds(pl.multiple_of(rank * rows, 16), rows)

    own_copy = pltpu.make_async_copy(
        ens.at[pl.ds(me * 2 * pairs, 2 * pairs)], ebuf.at[:, slot(me)], own_sem
    )
    staged = (
        (field_in, field),
        (loc_in, loc),
        (svert_in, svert),
        (taper_in, taper),
        (static_taper_in, static_taper),
        (sdev_in, sdev),
        (ids_in, ids),
        (value_in, value),
        (rinv_in, rinv),
        (horiz_in, horiz),
        (vert_in, vert),
    )
    stage = [
        pltpu.make_async_copy(src, dst, in_sem.at[q]) for q, (src, dst) in enumerate(staged)
    ]
    for copy in stage:
        copy.start()
    own_copy.start()
    lons = [lax.rem(lon + off, nlon) for off in range(1, nlon)]

    barrier = pltpu.get_barrier_semaphore()
    for peer in peers:
        pl.semaphore_signal(barrier, inc=1, device_id={"lev": peer}, device_id_type=MESH)
    for peer in lons:
        pl.semaphore_signal(barrier, inc=1, device_id={"lon": peer}, device_id_type=MESH)
    width = loc.shape[1]
    stage[0].wait()
    fsend[...] = field[...].astype(BF16)
    fgroup[slot(me)] = fsend[...]
    for copy in stage[1:]:
        copy.wait()
    for matrix, padded in ((loc, lpad), (svert, spad)):
        padded[...] = jnp.zeros_like(padded)
        padded[:levs, :width] = matrix[...]
    spart[...] = (sdev[...] * field[...]).astype(BF16)
    slots = ids.shape[1]
    lats = field.shape[1]
    folds = slots // 128
    for q in range(folds):
        vfold[q * levs : (q + 1) * levs] = vert[:, q * 128 : (q + 1) * 128]
    vsend[...] = vfold[...].astype(BF16)
    pl.semaphore_wait(barrier, nlev + nlon - 2)

    def land(which, rank):
        dst = (lg, fgroup, zs, vg)[which]
        return dst.at[rank] if which in (0, 3) else dst.at[slot(rank)]

    def small(which, off, peer, rank):
        return pltpu.make_async_remote_copy(
            src_ref=(lpad, fsend, smooth, vsend)[which],
            dst_ref=land(which, rank),
            send_sem=small_send.at[which, off],
            recv_sem=small_recv.at[which, rank],
            device_id={"lev": peer},
            device_id_type=MESH,
        )

    def relay(which, q, k):
        return pltpu.make_async_remote_copy(
            src_ref=land(which, far_ranks[q]),
            dst_ref=land(which, far_ranks[q]),
            send_sem=relay_send.at[which, q * hl + k],
            recv_sem=small_recv.at[which, far_ranks[q]],
            device_id={"lev": near_ranks[k]},
            device_id_type=MESH,
        )

    def gather_start(which):
        for off, peer in enumerate(peers):

            @pl.when((peer // hl == side) | (peer == other_gate))
            def _(off=off, peer=peer):
                small(which, off, peer, me).start()

    def gather_far(which):
        for q, rank in enumerate(far_ranks):
            small(which, 0, peers[0], rank).wait_recv()

            @pl.when(gate)
            def _(q=q):
                for k in range(hl - 1):
                    relay(which, q, k).start()

    def gather_near(which):
        for rank in near_ranks:
            small(which, 0, peers[0], rank).wait_recv()

    def gather_drain(which):
        for off, peer in enumerate(peers):

            @pl.when((peer // hl == side) | (peer == other_gate))
            def _(off=off, peer=peer):
                small(which, off, peer, me).wait_send()

        @pl.when(gate)
        def _():
            for q in range(hl):
                for k in range(hl - 1):
                    relay(which, q, k).wait_send()

    def ens_copy(off, peer, rank, c):
        return pltpu.make_async_remote_copy(
            src_ref=ens.at[peer * 2 * pairs + c],
            dst_ref=ebuf.at[c, slot(rank)],
            send_sem=ens_send.at[off, c],
            recv_sem=ens_recv.at[rank, c],
            device_id={"lev": peer},
            device_id_type=MESH,
        )

    def halo_copy(side_to, c, h, rank=None):
        lane = pl.ds(h * 128, 128)
        base = full + side_to * edge
        if rank is None:
            src, dst = pl.ds(0, edge), pl.ds(base, edge)
        else:
            first = pl.multiple_of(rank * strip, 16)
            src, dst = pl.ds(first, strip), pl.ds(base + first, strip)
        return pltpu.make_async_remote_copy(
            src_ref=hsend.at[side_to, c, src, lane],
            dst_ref=zbuf.at[c, dst, lane],
            send_sem=halo_send.at[side_to, 2 * c + h],
            recv_sem=halo_recv.at[side_to, 2 * c + h],
            device_id={"lon": (right, left)[side_to]},
            device_id_type=MESH,
        )

    def static_halo(side_to):
        return pltpu.make_async_remote_copy(
            src_ref=ssend.at[side_to],
            dst_ref=sbuf.at[pl.ds(rows + side_to * strip, strip)],
            send_sem=halo_send.at[side_to, 2 * pairs],
            recv_sem=halo_recv.at[side_to, 2 * pairs],
            device_id={"lon": (right, left)[side_to]},
            device_id_type=MESH,
        )

    def back_copy(off, peer):
        return pltpu.make_async_remote_copy(
            src_ref=accb.at[slot(peer)],
            dst_ref=rbuf.at[off],
            send_sem=back_send.at[off],
            recv_sem=back_recv.at[off],
            device_id={"lev": peer},
            device_id_type=MESH,
        )

    def part_copy(off, peer, rank):
        return pltpu.make_async_remote_copy(
            src_ref=part,
            dst_ref=parts.at[rank],
            send_sem=part_send.at[off],
            recv_sem=part_recv.at[off],
            device_id={"lev": peer},
            device_id_type=MESH,
        )

    def cost_copy(off, rank):
        return pltpu.make_async_remote_copy(
            src_ref=costs.at[lon],
            dst_ref=costs.at[rank],
            send_sem=cost_send.at[off],
            recv_sem=cost_recv.at[off],
            device_id={"lon": lons[off]},
            device_id_type=MESH,
        )

    def send_chunk(c, carry):
        for off, peer in enumerate(peers):
            ens_copy(off, peer, me, c).start()
        return carry

    def edges(values):
        lines = values.reshape(values.shape[0] // cols, cols, values.shape[1])
        span = values.shape[0] // cols * half
        to_right = lines[:, cols - half :].reshape(span, values.shape[1]).astype(BF16)
        to_left = lines[:, :half].reshape(span, values.shape[1]).astype(BF16)
        return to_right, to_left

    gather_start(1)
    gather_start(0)
    lax.fori_loop(0, 2 * pairs, send_chunk, 0)
    sbuf[:rows] = spart[...]
    ssend[0], ssend[1] = edges(spart[...].astype(F32))
    for side_to in range(2):
        static_halo(side_to).start()

    lg[me] = lpad[...]
    vg[me] = vsend[...]
    acc[...] = jnp.zeros_like(acc)

    def columns(count, inside):
        col = lax.broadcasted_iota(jnp.int32, (count, inside * 2), 1)
        inner = col < inside
        low = col < inside + inside // 2
        tail = jnp.where(low, col - inside, col - inside - inside // 2)
        level = jnp.where(inner, col // cols, tail // half)
        place = jnp.where(
            inner,
            half + col % cols,
            jnp.where(low, tail % half, half + cols + tail % half),
        )
        return level, place

    def banded(place, weights):
        spot = place - lax.broadcasted_iota(jnp.int32, place.shape, 0)
        tap = weights[...].astype(F32)
        band = jnp.zeros(place.shape, F32)
        for d in range(tap.shape[1]):
            band = jnp.where(spot == d, tap[:, d : d + 1], band)
        return band

    level, place = columns(cols, rows)
    band = banded(place, static_taper)
    for q in range(levs):
        sband[q * cols : (q + 1) * cols] = jnp.where(level == q, band, 0.0).astype(BF16)
    for side_to in range(2):
        static_halo(side_to).wait_recv()
    smooth[...] = jnp.dot(sband[...], sbuf[...], preferred_element_type=F32).astype(BF16)
    zs[slot(me)] = smooth[...]

    @pl.when(gate)
    def _():
        gather_start(2)
        gather_start(3)

    lanes = lpad.shape[1]
    level, place = columns(lanes, full)
    row = lax.broadcasted_iota(jnp.int32, (lanes, wide), 0)
    pick[...] = jnp.where(row == level, 1.0, 0.0).astype(BF16)
    tband[...] = banded(place[:cols], taper)

    padrows = lpad.shape[0]

    gather_far(1)
    gather_far(0)
    gather_near(1)
    gather_near(0)
    fbuf[...] = fgroup[...].astype(F32)

    def expand_loc(rank, carry):
        spread[...] = jnp.dot(lg[rank], pick[...], preferred_element_type=F32)

        def one(q, inner_carry):
            at = pl.ds(pl.multiple_of((rank * levs + q) * cols, 16), cols)
            w[at] = (spread[pl.ds(q, 1)] * tband[...]).astype(BF16)
            return inner_carry

        return lax.fori_loop(0, levs, one, carry)

    lax.fori_loop(0, nlev, expand_loc, 0)
    spread[:, :full] = jnp.dot(spad[...], pick[:, :full], preferred_element_type=F32)
    same = lax.broadcasted_iota(jnp.int32, (cols, full), 1) % cols == (
        lax.broadcasted_iota(jnp.int32, (cols, full), 0)
    )

    def expand_static(q, carry):
        at = pl.ds(pl.multiple_of(q * cols, 16), cols)
        ws[at] = jnp.where(same, spread[pl.ds(q, 1), :full], 0.0).astype(BF16)
        return carry

    lax.fori_loop(0, levs, expand_static, 0)

    nby = lats // GROUP
    nbx = cols // LINE
    levels = nlev * levs
    live = ids[...] >= 0
    local_ids = ids[...] - lon * (nbx * nby)
    by = jnp.where(live, local_ids % nby, -1)
    bx = jnp.where(live, local_ids // nby, -1)
    hturn[...] = horiz[...].T

    def spread_horiz(s, carry):
        line = hturn[pl.ds(pl.multiple_of(s * GROUP, GROUP), GROUP)]
        block = jnp.concatenate([jnp.where(by == q, line, 0.0) for q in range(nby)], axis=0)
        at = pl.ds(pl.multiple_of(s * lats, lats), lats)
        hcol[at] = block.astype(BF16)
        hrow[:, at] = block.T.astype(BF16)
        return carry

    lax.fori_loop(0, LINE, spread_horiz, 0)

    own_copy.wait()

    tile = full // 3 if full % 48 == 0 else full

    def enter(c, h, rank):
        lane = slice(h * 128, (h + 1) * 128)
        product = ebuf[2 * c + h, slot(rank)].astype(F32) * fbuf[slot(rank)]
        at = pl.ds(pl.multiple_of(rank * strip, 16), strip)
        hsend[0, c, at, lane], hsend[1, c, at, lane] = edges(product)
        zbuf[c, slot(rank), lane] = product.astype(BF16)
        for side_to in range(2):
            halo_copy(side_to, c, h, rank).start()

    gates = (hl - 1, hl)

    def arrive(c, h, rank):
        ens_copy(0, peers[0], rank, 2 * c + h).wait_recv()

    def chunk(t, carry):
        @pl.when(t < pairs)
        def _():
            for h in range(2):
                enter(t, h, me)
                for rank in range(nlev):
                    if rank not in gates:

                        @pl.when(rank != me)
                        def _(h=h, rank=rank):
                            arrive(t, h, rank)
                            enter(t, h, rank)

        c = t - lead

        @pl.when((c >= 0) & (c < pairs))
        def _():
            for h in range(2):
                for rank in gates:

                    @pl.when(rank != me)
                    def _(h=h, rank=rank):
                        arrive(c, h, rank)
                        enter(c, h, rank)

                if h == 0:

                    @pl.when((c == pairs - 1) & jnp.logical_not(gate))
                    def _():
                        gather_start(2)
                        gather_start(3)

        @pl.when((c == pairs) & gate)
        def _():
            gather_far(2)
            gather_far(3)

        @pl.when(c >= 1)
        def _():
            d = c - 1
            for h in range(2):
                for side_to in range(2):
                    halo_copy(side_to, d, h).wait_recv()

            def piece(q, inner_carry):
                at = pl.ds(pl.multiple_of(q * tile, 16), tile)
                zv = jnp.dot(w[at], zbuf[d], preferred_element_type=F32)
                acc[at] += (
                    ebuf[2 * d, at].astype(F32) * zv[:, :128]
                    + ebuf[2 * d + 1, at].astype(F32) * zv[:, 128:]
                )
                return inner_carry

            lax.fori_loop(0, full // tile, piece, 0)

        return carry

    lax.fori_loop(0, pairs + lead + 1, chunk, 0)

    accb[...] = acc[...].astype(BF16)
    for off, peer in enumerate(peers):
        back_copy(off, peer).start()

    @pl.when(jnp.logical_not(gate))
    def _():
        gather_far(2)
        gather_far(3)

    gather_near(2)
    gather_near(3)
    for rank in range(nlev):
        folded = vg[rank].astype(F32)
        for p in range(folds):
            piece = folded[p * levs : (p + 1) * levs]
            lane = slice(p * 128, (p + 1) * 128)
            for q in range(nbx):
                at = slice(q * levels + rank * levs, q * levels + (rank + 1) * levs)
                vx[at, lane] = jnp.where(bx[:, lane] == q, piece, 0.0)
    static = jnp.dot(ws[...], zs[...], preferred_element_type=F32)
    acc[slot(me)] += (static_weight / ens_weight) * sdev[...] * static

    for q in range(nbx):
        for s in range(LINE):
            cells[q * levels : (q + 1) * levels, s * lats : (s + 1) * lats] = acc[
                pl.ds(q * LINE + s, levels, stride=cols)
            ]
    projected = jnp.dot(cells[...].astype(BF16), hcol[...], preferred_element_type=F32)
    mine = ens_weight * jnp.sum(projected * vx[...], axis=0, keepdims=True)
    part[...] = mine
    parts[me] = mine
    for off, peer in enumerate(peers):
        part_copy(off, peer, me).start()
    for off, rank in enumerate(sources):
        part_copy(off, peers[off], rank).wait_recv()
    hx = parts[0]
    for rank in range(1, nlev):
        hx = hx + parts[rank]
    miss = hx - value[...]
    dep = jnp.where(live, rinv[...] * miss, 0.0)
    terms = 0.5 * dep * miss
    folded = terms[:, :128]
    for q in range(1, slots // 128):
        folded = folded + terms[:, q * 128 : (q + 1) * 128]
    costs[lon] = folded
    for off in range(nlon - 1):
        cost_copy(off, lon).start()
    held = -(-levs // 8) * 8
    weighted = jnp.concatenate(
        [vert[...] * (dep / ens_weight), jnp.zeros((held - levs, slots), F32)], axis=0
    )
    chosen = jnp.concatenate([jnp.where(bx == q, weighted, 0.0) for q in range(nbx)], axis=0)
    sums = jnp.dot(chosen.astype(BF16), hrow[...], preferred_element_type=F32)
    for q in range(nbx):
        for s in range(LINE):
            both[1, pl.ds(q * LINE + s, levs, stride=cols)] = sums[
                q * held : q * held + levs, s * lats : (s + 1) * lats
            ]
    total = acc[slot(me)]
    for off, peer in enumerate(peers):
        back_copy(off, peer).wait_recv()
        total = total + rbuf[off].astype(F32)
    both[0] = total
    for off in range(nlon - 1):
        cost_copy(off, lax.rem(lon + nlon - off - 1, nlon)).wait_recv()
    total_cost = costs[0]
    for rank in range(1, nlon):
        total_cost = total_cost + costs[rank]
    cost[...] = jnp.sum(total_cost, axis=1, keepdims=True)

    for off, peer in enumerate(peers):
        part_copy(off, peer, me).wait_send()
    for off in range(nlon - 1):
        cost_copy(off, lon).wait_send()
    for which in range(4):
        gather_drain(which)
    for off, peer in enumerate(peers):
        back_copy(off, peer).wait_send()
    for side_to in range(2):
        static_halo(side_to).wait_send()

    def drain(c, carry):
        for h in range(2):
            for off, peer in enumerate(peers):
                ens_copy(off, peer, me, 2 * c + h).wait_send()
            for side_to in range(2):
                halo_copy(side_to, c, h).wait_send()
        return carry

    lax.fori_loop(0, pairs, drain, 0)


def body(
    nlev,
    nlon,
    field,
    ens,
    sdev,
    lon_taper,
    static_taper,
    loc_vert,
    static_vert,
    obs_block,
    obs_value,
    obs_rinv,
    obs_horiz,
    obs_vert,
):
    members, levs, cols, lats = ens.shape
    half = lon_taper.shape[0] // 2
    pairs = members // nlev // 2
    rows = levs * cols
    full = nlev * rows
    edge = nlev * levs * half
    wide = full + 2 * edge
    slots = obs_block.shape[0]
    padrows = -(-levs // 16) * 16
    taps = lon_taper.shape[0]
    width = loc_vert.shape[1]
    picks = cols // LINE * nlev * levs
    hl = nlev // 2
    vmem = pl.BlockSpec(memory_space=pltpu.VMEM)
    dma = pltpu.SemaphoreType.DMA
    both, obs_cost = pl.pallas_call(
        functools.partial(main_kernel, (nlev, nlon, levs, cols, half, pairs)),
        out_shape=(
            jax.ShapeDtypeStruct((2, rows, lats), F32),
            jax.ShapeDtypeStruct((1, 1), F32),
        ),
        in_specs=[pl.BlockSpec(memory_space=pl.ANY)] * 12,
        out_specs=(vmem, vmem),
        scratch_shapes=[
            pltpu.VMEM((rows, lats), F32),
            pltpu.VMEM((rows, lats), F32),
            pltpu.VMEM((1, taps), BF16),
            pltpu.VMEM((1, taps), BF16),
            pltpu.VMEM((levs, width), BF16),
            pltpu.VMEM((levs, width), BF16),
            pltpu.VMEM((1, slots), jnp.int32),
            pltpu.VMEM((1, slots), F32),
            pltpu.VMEM((1, slots), F32),
            pltpu.VMEM((slots, lats), F32),
            pltpu.VMEM((levs, slots), F32),
            pltpu.VMEM((2 * pairs, full, lats), BF16),
            pltpu.VMEM((pairs, wide, 2 * lats), BF16),
            pltpu.VMEM((2, pairs, edge, 2 * lats), BF16),
            pltpu.VMEM((rows, lats), BF16),
            pltpu.VMEM((full, lats), BF16),
            pltpu.VMEM((full, lats), F32),
            pltpu.VMEM((rows, lats), BF16),
            pltpu.VMEM((rows, 2 * rows), BF16),
            pltpu.VMEM((2 * rows, lats), BF16),
            pltpu.VMEM((2, levs * half, lats), BF16),
            pltpu.VMEM((rows, lats), BF16),
            pltpu.VMEM((full, lats), BF16),
            pltpu.VMEM((padrows, 128), BF16),
            pltpu.VMEM((padrows, 128), BF16),
            pltpu.VMEM((nlev, padrows, 128), BF16),
            pltpu.VMEM((padrows, wide), F32),
            pltpu.VMEM((full, wide), BF16),
            pltpu.VMEM((rows, full), BF16),
            pltpu.VMEM((128, wide), BF16),
            pltpu.VMEM((cols, wide), F32),
            pltpu.VMEM((full, lats), F32),
            pltpu.VMEM((full, lats), BF16),
            pltpu.VMEM((nlev - 1, rows, lats), BF16),
            pltpu.VMEM((lats, slots), F32),
            pltpu.VMEM((LINE * lats, slots), BF16),
            pltpu.VMEM((slots, LINE * lats), BF16),
            pltpu.VMEM((picks, LINE * lats), F32),
            pltpu.VMEM((levs * slots // 128, 128), F32),
            pltpu.VMEM((levs * slots // 128, 128), BF16),
            pltpu.VMEM((nlev, levs * slots // 128, 128), BF16),
            pltpu.VMEM((picks, slots), F32),
            pltpu.VMEM((1, slots), F32),
            pltpu.VMEM((nlev, 1, slots), F32),
            pltpu.VMEM((nlon, 1, 128), F32),
            dma,
            dma((11,)),
            dma((nlev - 1, 2 * pairs)),
            dma((nlev, 2 * pairs)),
            dma((2, 2 * pairs + 1)),
            dma((2, 2 * pairs + 1)),
            dma((4, nlev - 1)),
            dma((4, nlev)),
            dma((4, hl * hl)),
            dma((nlev - 1,)),
            dma((nlev - 1,)),
            dma((nlev - 1,)),
            dma((nlev - 1,)),
            dma((nlon - 1,)),
            dma((nlon - 1,)),
        ],
        compiler_params=pltpu.CompilerParams(
            collective_id=0, has_side_effects=True, vmem_limit_bytes=63 * 1024 * 1024
        ),
        name="covariance",
    )(
        ens.reshape(members, rows, lats),
        field.reshape(rows, lats),
        sdev.reshape(rows, lats),
        lon_taper.reshape(1, -1),
        static_taper.reshape(1, -1),
        loc_vert,
        static_vert,
        obs_block.reshape(1, slots),
        obs_value.reshape(1, slots),
        obs_rinv.reshape(1, slots),
        obs_horiz,
        obs_vert.T,
    )
    shape = (levs, cols, lats)
    increment, adjoint_field = ens_weight * both[0], ens_weight * both[1]
    return (increment.reshape(shape), adjoint_field.reshape(shape), obs_cost[0, 0])


def solution(mesh):
    return jax.shard_map(
        functools.partial(body, mesh.shape["lev"], mesh.shape["lon"]),
        mesh=mesh,
        in_specs=(
            P("lev", "lon", None),
            P(None, "lev", "lon", None),
            P("lev", "lon", None),
            P(),
            P(),
            P("lev", None),
            P("lev", None),
            P("lon"),
            P("lon"),
            P("lon"),
            P("lon", None),
            P("lon", "lev"),
        ),
        out_specs=(P("lev", "lon", None), P("lev", "lon", None), P()),
        check_vma=False,
    )
```

time: 184 us -> 171 us (0.929)
  Pallas kernels: 179 us -> 166 us
  local copies, waits for them, and re-layouts: 3.16 us -> 0 us
    pallas_call x1, Pallas kernels: 179 us -> 166 us  [body(): pl.pallas_call(functools.partial(main_kernel, (nlev, nlon, levs, cols, ha...]
    unnamed x2 -> x0, local copies, waits for them, and re-layouts: 3.16 us -> none
where the time goes in v1:
time: 171 us
  Pallas kernels  166 us (97%)
  between operations  2.46 us (1%)
  other arithmetic  1.72 us (1%)
    pallas_call x1, Pallas kernels, body(): pl.pallas_call(functools.partial(main_kernel, (nlev, nlon, levs, cols, ha...  166 us

profile of v1, /device:TPU:0, one launch (start us, length us, event | category | flops | bytes accessed | tf_op | source)
XLA Modules:
  0.0 170.7 jit_solution(15809845512001144711)
XLA Ops:
  0.6 166.5 %covariance.1 = (f32[2,288,128]{2,1,0:T(8,128)}, f32[1,1]{1,0:T(1,128)}) custom-call(bf16[80,288,128]{2,1,0:T(8,128)(2,1)} %bitcast.12, f32[288,128]{1,0:T(8,128)} %bitcast.13, f32[288,128]{1,0:T(8,128)} %bitcast.14, bf16[1,17]{1,0:T(2,128)(2,1)} %bitcast.21, bf16[1,17]{1,0:T(2,128)(2,1)} %bitcast.22, bf16[18,72]{1,0:T(8,128)(2,1)} %loc_in.1, ...), custom_call_target="tpu_custom_call" | custom-call | tf_op jit(solution)/shard_map/covariance/pallas_call | solution.py:607
  167.1 1.7 %slice_multiply_fusion = (f32[1,288,128]{2,1,0:T(8,128)}, f32[1,288,128]{2,1,0:T(8,128)}) fusion(f32[2,288,128]{2,1,0:T(8,128)} %get-tuple-element.5), kind=kLoop, calls=%fused_computation | loop fusion | flops 73728 | bytes 589824 | tf_op jit(solution)/shard_map/mul | solution.py:696

commit v2 on v1

--- a/solution.py
+++ b/solution.py
@@ -16,7 +16,6 @@
 
 LINE = 8
 GROUP = 16
-LEAD = 0
 
 
 def main_kernel(
@@ -101,7 +100,6 @@
     full = nlev * rows
     edge = nlev * levs * half
     wide = full + 2 * edge
-    lead = min(LEAD, pairs)
     strip = levs * half
     hl = nlev // 2
     me = lax.axis_index("lev")
@@ -233,7 +231,7 @@
         )
 
     def halo_copy(side_to, c, h, rank=None):
-        lane = pl.ds(h * 128, 128)
+        lane = pl.ds(pl.multiple_of(h * 128, 128), 128)
         base = full + side_to * edge
         if rank is None:
             src, dst = pl.ds(0, edge), pl.ds(base, edge)
@@ -303,6 +301,7 @@
 
     gather_start(1)
     gather_start(0)
+    gather_start(3)
     lax.fori_loop(0, 2 * pairs, send_chunk, 0)
     sbuf[:rows] = spart[...]
     ssend[0], ssend[1] = edges(spart[...].astype(F32))
@@ -346,7 +345,6 @@
     @pl.when(gate)
     def _():
         gather_start(2)
-        gather_start(3)
 
     lanes = lpad.shape[1]
     level, place = columns(lanes, full)
@@ -404,93 +402,7 @@
 
     lax.fori_loop(0, LINE, spread_horiz, 0)
 
-    own_copy.wait()
-
-    tile = full // 3 if full % 48 == 0 else full
-
-    def enter(c, h, rank):
-        lane = slice(h * 128, (h + 1) * 128)
-        product = ebuf[2 * c + h, slot(rank)].astype(F32) * fbuf[slot(rank)]
-        at = pl.ds(pl.multiple_of(rank * strip, 16), strip)
-        hsend[0, c, at, lane], hsend[1, c, at, lane] = edges(product)
-        zbuf[c, slot(rank), lane] = product.astype(BF16)
-        for side_to in range(2):
-            halo_copy(side_to, c, h, rank).start()
-
-    gates = (hl - 1, hl)
-
-    def arrive(c, h, rank):
-        ens_copy(0, peers[0], rank, 2 * c + h).wait_recv()
-
-    def chunk(t, carry):
-        @pl.when(t < pairs)
-        def _():
-            for h in range(2):
-                enter(t, h, me)
-                for rank in range(nlev):
-                    if rank not in gates:
-
-                        @pl.when(rank != me)
-                        def _(h=h, rank=rank):
-                            arrive(t, h, rank)
-                            enter(t, h, rank)
-
-        c = t - lead
-
-        @pl.when((c >= 0) & (c < pairs))
-        def _():
-            for h in range(2):
-                for rank in gates:
-
-                    @pl.when(rank != me)
-                    def _(h=h, rank=rank):
-                        arrive(c, h, rank)
-                        enter(c, h, rank)
-
-                if h == 0:
-
-                    @pl.when((c == pairs - 1) & jnp.logical_not(gate))
-                    def _():
-                        gather_start(2)
-                        gather_start(3)
-
-        @pl.when((c == pairs) & gate)
-        def _():
-            gather_far(2)
-            gather_far(3)
-
-        @pl.when(c >= 1)
-        def _():
-            d = c - 1
-            for h in range(2):
-                for side_to in range(2):
-                    halo_copy(side_to, d, h).wait_recv()
-
-            def piece(q, inner_carry):
-                at = pl.ds(pl.multiple_of(q * tile, 16), tile)
-                zv = jnp.dot(w[at], zbuf[d], preferred_element_type=F32)
-                acc[at] += (
-                    ebuf[2 * d, at].astype(F32) * zv[:, :128]
-                    + ebuf[2 * d + 1, at].astype(F32) * zv[:, 128:]
-                )
-                return inner_carry
-
-            lax.fori_loop(0, full // tile, piece, 0)
-
-        return carry
-
-    lax.fori_loop(0, pairs + lead + 1, chunk, 0)
-
-    accb[...] = acc[...].astype(BF16)
-    for off, peer in enumerate(peers):
-        back_copy(off, peer).start()
-
-    @pl.when(jnp.logical_not(gate))
-    def _():
-        gather_far(2)
-        gather_far(3)
-
-    gather_near(2)
+    gather_far(3)
     gather_near(3)
     for rank in range(nlev):
         folded = vg[rank].astype(F32)
@@ -500,6 +412,76 @@
             for q in range(nbx):
                 at = slice(q * levels + rank * levs, q * levels + (rank + 1) * levs)
                 vx[at, lane] = jnp.where(bx[:, lane] == q, piece, 0.0)
+
+    own_copy.wait()
+
+    tile = full // 3 if full % 48 == 0 else full
+
+    steps = 2 * nlev
+
+    def enter(e, c):
+        late = e >= steps
+        h = jnp.where(late, (e - steps) // 2, e // nlev)
+        rank = jnp.where(late, hl - 1 + (e - steps) % 2, e % nlev)
+        gated = (rank == hl - 1) | (rank == hl)
+        mine = rank == me
+
+        @pl.when(jnp.where(late, jnp.logical_not(mine), jnp.logical_not(gated) | mine))
+        def _():
+            @pl.when(jnp.logical_not(mine))
+            def _():
+                ens_copy(0, peers[0], rank, 2 * c + h).wait_recv()
+
+            lane = pl.ds(pl.multiple_of(h * 128, 128), 128)
+            product = ebuf[2 * c + h, slot(rank)].astype(F32) * fbuf[slot(rank)]
+            at = pl.ds(pl.multiple_of(rank * strip, 16), strip)
+            hsend[0, c, at, lane], hsend[1, c, at, lane] = edges(product)
+            zbuf[c, slot(rank), lane] = product.astype(BF16)
+            for side_to in range(2):
+                halo_copy(side_to, c, h, rank).start()
+
+        return c
+
+    def chunk(c, carry):
+        @pl.when(c < pairs)
+        def _():
+            lax.fori_loop(0, steps + 4, enter, c)
+
+            @pl.when((c == pairs - 1) & jnp.logical_not(gate))
+            def _():
+                gather_start(2)
+
+        @pl.when((c == pairs) & gate)
+        def _():
+            gather_far(2)
+
+        @pl.when(c >= 1)
+        def _():
+            d = c - 1
+            for h in range(2):
+                for side_to in range(2):
+                    halo_copy(side_to, d, h).wait_recv()
+
+            def piece(q, inner_carry):
+                at = pl.ds(pl.multiple_of(q * tile, 16), tile)
+                zv = jnp.dot(w[at], zbuf[d], preferred_element_type=F32)
+                acc[at] += (
+                    ebuf[2 * d, at].astype(F32) * zv[:, :128]
+                    + ebuf[2 * d + 1, at].astype(F32) * zv[:, 128:]
+                )
+                return inner_carry
+
+            lax.fori_loop(0, full // tile, piece, 0)
+
+        return carry
+
+    lax.fori_loop(0, pairs + 1, chunk, 0)
+
+    @pl.when(jnp.logical_not(gate))
+    def _():
+        gather_far(2)
+
+    gather_near(2)
     static = jnp.dot(ws[...], zs[...], preferred_element_type=F32)
     acc[slot(me)] += (static_weight / ens_weight) * sdev[...] * static
 
@@ -514,6 +496,9 @@
     parts[me] = mine
     for off, peer in enumerate(peers):
         part_copy(off, peer, me).start()
+    accb[...] = acc[...].astype(BF16)
+    for off, peer in enumerate(peers):
+        back_copy(off, peer).start()
     for off, rank in enumerate(sources):
         part_copy(off, peers[off], rank).wait_recv()
     hx = parts[0]

time: 171 us -> 165 us (0.965)
  Pallas kernels: 166 us -> 160 us
    pallas_call x1, Pallas kernels: 166 us -> 160 us  [body(): pl.pallas_call(functools.partial(main_kernel, (nlev, nlon, levs, cols, ha...]
where the time goes in v2:
time: 165 us
  Pallas kernels  160 us (97%)
  between operations  2.46 us (1%)
  other arithmetic  1.72 us (1%)
    pallas_call x1, Pallas kernels, body(): pl.pallas_call(functools.partial(main_kernel, (nlev, nlon, levs, cols, ha...  160 us

profile of v2, /device:TPU:0, one launch (start us, length us, event | category | flops | bytes accessed | tf_op | source)
XLA Modules:
  0.0 164.6 jit_solution(14893989122707703147)
XLA Ops:
  0.6 160.5 %covariance.1 = (f32[2,288,128]{2,1,0:T(8,128)}, f32[1,1]{1,0:T(1,128)}) custom-call(bf16[80,288,128]{2,1,0:T(8,128)(2,1)} %bitcast.12, f32[288,128]{1,0:T(8,128)} %bitcast.13, f32[288,128]{1,0:T(8,128)} %bitcast.14, bf16[1,17]{1,0:T(2,128)(2,1)} %bitcast.21, bf16[1,17]{1,0:T(2,128)(2,1)} %bitcast.22, bf16[18,72]{1,0:T(8,128)(2,1)} %loc_in.1, ...), custom_call_target="tpu_custom_call" | custom-call | tf_op jit(solution)/shard_map/covariance/pallas_call | solution.py:592
  161.1 1.7 %slice_multiply_fusion = (f32[1,288,128]{2,1,0:T(8,128)}, f32[1,288,128]{2,1,0:T(8,128)}) fusion(f32[2,288,128]{2,1,0:T(8,128)} %get-tuple-element.5), kind=kLoop, calls=%fused_computation | loop fusion | flops 73728 | bytes 589824 | tf_op jit(solution)/shard_map/mul | solution.py:681

commit v3 on v2

--- a/solution.py
+++ b/solution.py
@@ -32,7 +32,7 @@
     rinv_in,
     horiz_in,
     vert_in,
-    both,
+    both_out,
     cost,
     field,
     sdev,
@@ -79,7 +79,9 @@
     part,
     parts,
     costs,
+    both,
     own_sem,
+    out_sem,
     in_sem,
     ens_send,
     ens_recv,
@@ -119,6 +121,9 @@
     own_copy = pltpu.make_async_copy(
         ens.at[pl.ds(me * 2 * pairs, 2 * pairs)], ebuf.at[:, slot(me)], own_sem
     )
+    leave = [
+        pltpu.make_async_copy(both.at[q], both_out.at[q], out_sem.at[q]) for q in range(2)
+    ]
     staged = (
         (field_in, field),
         (loc_in, loc),
@@ -129,15 +134,12 @@
         (ids_in, ids),
         (value_in, value),
         (rinv_in, rinv),
+        (vert_in, vert),
         (horiz_in, horiz),
-        (vert_in, vert),
     )
     stage = [
         pltpu.make_async_copy(src, dst, in_sem.at[q]) for q, (src, dst) in enumerate(staged)
     ]
-    for copy in stage:
-        copy.start()
-    own_copy.start()
     lons = [lax.rem(lon + off, nlon) for off in range(1, nlon)]
 
     barrier = pltpu.get_barrier_semaphore()
@@ -145,11 +147,13 @@
         pl.semaphore_signal(barrier, inc=1, device_id={"lev": peer}, device_id_type=MESH)
     for peer in lons:
         pl.semaphore_signal(barrier, inc=1, device_id={"lon": peer}, device_id_type=MESH)
+    for copy in stage[:-1]:
+        copy.start()
     width = loc.shape[1]
     stage[0].wait()
     fsend[...] = field[...].astype(BF16)
     fgroup[slot(me)] = fsend[...]
-    for copy in stage[1:]:
+    for copy in stage[1:-1]:
         copy.wait()
     for matrix, padded in ((loc, lpad), (svert, spad)):
         padded[...] = jnp.zeros_like(padded)
@@ -303,6 +307,8 @@
     gather_start(0)
     gather_start(3)
     lax.fori_loop(0, 2 * pairs, send_chunk, 0)
+    stage[-1].start()
+    own_copy.start()
     sbuf[:rows] = spart[...]
     ssend[0], ssend[1] = edges(spart[...].astype(F32))
     for side_to in range(2):
@@ -390,6 +396,7 @@
     local_ids = ids[...] - lon * (nbx * nby)
     by = jnp.where(live, local_ids % nby, -1)
     bx = jnp.where(live, local_ids // nby, -1)
+    stage[-1].wait()
     hturn[...] = horiz[...].T
 
     def spread_horiz(s, carry):
@@ -524,11 +531,13 @@
             both[1, pl.ds(q * LINE + s, levs, stride=cols)] = sums[
                 q * held : q * held + levs, s * lats : (s + 1) * lats
             ]
+    leave[1].start()
     total = acc[slot(me)]
     for off, peer in enumerate(peers):
         back_copy(off, peer).wait_recv()
         total = total + rbuf[off].astype(F32)
     both[0] = total
+    leave[0].start()
     for off in range(nlon - 1):
         cost_copy(off, lax.rem(lon + nlon - off - 1, nlon)).wait_recv()
     total_cost = costs[0]
@@ -536,6 +545,8 @@
         total_cost = total_cost + costs[rank]
     cost[...] = jnp.sum(total_cost, axis=1, keepdims=True)
 
+    for copy in leave:
+        copy.wait()
     for off, peer in enumerate(peers):
         part_copy(off, peer, me).wait_send()
     for off in range(nlon - 1):
@@ -596,7 +607,7 @@
             jax.ShapeDtypeStruct((1, 1), F32),
         ),
         in_specs=[pl.BlockSpec(memory_space=pl.ANY)] * 12,
-        out_specs=(vmem, vmem),
+        out_specs=(pl.BlockSpec(memory_space=pl.ANY), vmem),
         scratch_shapes=[
             pltpu.VMEM((rows, lats), F32),
             pltpu.VMEM((rows, lats), F32),
@@ -643,7 +654,9 @@
             pltpu.VMEM((1, slots), F32),
             pltpu.VMEM((nlev, 1, slots), F32),
             pltpu.VMEM((nlon, 1, 128), F32),
+            pltpu.VMEM((2, rows, lats), F32),
             dma,
+            dma((2,)),
             dma((11,)),
             dma((nlev - 1, 2 * pairs)),
             dma((nlev, 2 * pairs)),

time: 165 us -> 165 us (level)
  no operation moved by 1% of the time
where the time goes in v3:
time: 165 us
  Pallas kernels  160 us (97%)
  between operations  2.46 us (1%)
  other arithmetic  1.72 us (1%)
    pallas_call x1, Pallas kernels, body(): pl.pallas_call(functools.partial(main_kernel, (nlev, nlon, levs, cols, ha...  160 us

profile of v3, /device:TPU:0, one launch (start us, length us, event | category | flops | bytes accessed | tf_op | source)
XLA Modules:
  0.0 164.5 jit_solution(15944292664079513007)
XLA Ops:
  0.6 160.3 %covariance.1 = (f32[2,288,128]{2,1,0:T(8,128)}, f32[1,1]{1,0:T(1,128)}) custom-call(bf16[80,288,128]{2,1,0:T(8,128)(2,1)} %bitcast.12, f32[288,128]{1,0:T(8,128)} %bitcast.13, f32[288,128]{1,0:T(8,128)} %bitcast.14, bf16[1,17]{1,0:T(2,128)(2,1)} %bitcast.21, bf16[1,17]{1,0:T(2,128)(2,1)} %bitcast.22, bf16[18,72]{1,0:T(8,128)(2,1)} %loc_in.1, ...), custom_call_target="tpu_custom_call" | custom-call | tf_op jit(solution)/shard_map/covariance/pallas_call | solution.py:603
  161.0 1.7 %slice_multiply_fusion = (f32[1,288,128]{2,1,0:T(8,128)}, f32[1,288,128]{2,1,0:T(8,128)}) fusion(f32[2,288,128]{2,1,0:T(8,128)} %get-tuple-element.5), kind=kLoop, calls=%fused_computation | loop fusion | flops 73728 | bytes 589824 | tf_op jit(solution)/shard_map/mul | solution.py:694
